TPU v7x, 256 devices: a whole 4x4x8 slice. The times are simulated.
256 devices in a mesh: grp: 8 (over y, x_lo), seq: 32 (over x_hi, z, core).
Axes of the slice: x: 4 (x_hi: 2, x_lo: 2; x = x_hi * 2 + x_lo), y: 4, z: 8, core: 2. Of those that a mesh axis runs over, the one named last changes fastest.
Arguments:
- queries: bfloat16 [16, 1024, 8192], P('grp', 'seq'), parts along dimension 0, may hold values from -400 to 400
- stretch_keys: bfloat16 [16, 1024, 1024], P('grp', 'seq'), parts along dimension 0, may hold values from -6 to 6
- stretch_values: bfloat16 [16, 1024, 1024], P('grp', 'seq'), parts along dimension 0, may hold values from -6 to 6
- cache_keys: bfloat16 [16, 2048, 1024], P('grp', 'seq'), parts along dimension 0, may hold values from -6 to 6
- cache_values: bfloat16 [16, 2048, 1024], P('grp', 'seq'), parts along dimension 0, may hold values from -6 to 6
- prefix_len: int32 [16], P('grp'), parts along dimension 0, may hold values from 16 to 2048, as said below
Outputs:
- attention: bfloat16 [16, 1024, 8192], P('grp', 'seq'), parts along dimension 0
- prefix_bounds: bfloat16 [16, 128, 2048], P('grp', 'seq'), parts along dimension 0
- stretch_bounds: bfloat16 [16, 64, 2048], P('grp', 'seq'), parts along dimension 0
There are 8 independent parts, one for each index of `grp`. A program takes and returns all parts, laid end to end along the dimension named above; each array names one. Nothing has to cross between parts.
Inputs may be any that keep to these rules, and one draw needn't show every extreme that they name: `prefix_len`: multiples of 16; some sequence of every group has 2048.
All inputs are finite; a program needn't handle non-finite values.
Results may differ from a plain program's by a relative error of at most 0.006.
Values may be sent and summed in bfloat16 or wider, within the bound.
A program may use at most 128 MiB of HBM per device.

v0:
```python
import math

import jax
import jax.numpy as jnp
from jax import lax
from jax.sharding import PartitionSpec as P

HQ = 64
HK = 8
DH = 128
PAGE = 16


def side_by_side(arrays, axis, dim, along):
    both = jnp.concatenate(arrays, axis=along)
    filled, at, gathered = (lax.all_gather(both, axis, axis=dim, tiled=True), 0, [])
    for a in arrays:
        gathered.append(lax.slice_in_dim(filled, at, at + a.shape[along], axis=along))
        at += a.shape[along]
    return tuple(gathered)


def pick_block(length):
    for candidate in range(min(length, 512), 0, -1):
        if length % candidate == 0:
            return candidate
    return 1


def online(state, query_rows, query_pos, key_rows, value_rows, key_pos, from_cache, prefix_len):
    seqs, rows, _ = query_rows.shape
    group = HQ // HK
    factor = 1.0 / math.sqrt(DH)
    length = key_rows.shape[1]
    block = pick_block(length)
    steps_count = length // block
    shaped_query = query_rows.reshape(seqs, rows, HK, group, DH)
    key_blocks = jnp.moveaxis(key_rows.reshape(seqs, steps_count, block, HK, DH), 1, 0)
    value_blocks = jnp.moveaxis(value_rows.reshape(seqs, steps_count, block, HK, DH), 1, 0)
    pos_blocks = key_pos.reshape(steps_count, block)
    cache_blocks = from_cache.reshape(steps_count, block)
    top_length = jnp.max(prefix_len)
    top_query = jnp.max(query_pos)

    def one_step(current, pieces):
        key_part, value_part, pos_part, cache_part = pieces

        def compute(carried):
            running_top, running_sum, running_acc = carried
            scores = (
                jnp.einsum(
                    "srhgd,skhd->srhgk", shaped_query, key_part, preferred_element_type=jnp.float32
                )
                * factor
            )
            live = jnp.where(
                cache_part[None, None, :],
                pos_part[None, None, :] < prefix_len[:, None, None],
                pos_part[None, None, :] <= query_pos[None, :, None],
            )
            live = live[:, :, None, None, :]
            new_top = jnp.maximum(running_top, jnp.max(jnp.where(live, scores, -1e30), axis=-1))
            weights = jnp.where(live, jnp.exp(scores - new_top[..., None]), 0.0)
            shrink = jnp.exp(running_top - new_top)
            new_sum = running_sum * shrink + jnp.sum(weights, axis=-1)
            new_acc = running_acc * shrink[..., None] + jnp.einsum(
                "srhgk,skhd->srhgd",
                weights.astype(jnp.bfloat16),
                value_part,
                preferred_element_type=jnp.float32,
            )
            return (new_top, new_sum, new_acc)

        useful = jnp.any(jnp.where(cache_part, pos_part < top_length, pos_part <= top_query))
        return (lax.cond(useful, compute, lambda carried: carried, current), None)

    result, _ = lax.scan(one_step, state, (key_blocks, value_blocks, pos_blocks, cache_blocks))
    return result


def page_bounds(key_rows, live_pages):
    seqs, rows, width = key_rows.shape
    shaped = key_rows.reshape(seqs, rows // PAGE, PAGE, width)
    joined = jnp.concatenate([jnp.min(shaped, axis=2), jnp.max(shaped, axis=2)], axis=2)
    return jnp.where(live_pages[:, :, None], joined, jnp.zeros_like(joined))


def on_device(queries, stretch_keys, stretch_values, cache_keys, cache_values, prefix_len):
    seqs, ch_rows, _ = queries.shape
    pre_rows = cache_keys.shape[1]
    own_index = lax.axis_index("seq")
    group = HQ // HK
    groups = ((queries, own_index * ch_rows + jnp.arange(ch_rows, dtype=jnp.int32)),)
    states = tuple(
        (
            (
                jnp.full((seqs, entry[0].shape[1], HK, group), -1e30, jnp.float32),
                jnp.zeros((seqs, entry[0].shape[1], HK, group), jnp.float32),
                jnp.zeros((seqs, entry[0].shape[1], HK, group, DH), jnp.float32),
            )
            for entry in groups
        )
    )

    def absorb(current, key_rows, value_rows, key_pos, from_cache):
        return tuple(
            (
                online(
                    state, entry[0], entry[1], key_rows, value_rows, key_pos, from_cache, prefix_len
                )
                for state, entry in zip(current, groups)
            )
        )

    old_keys, old_values = (
        lax.all_gather(cache_keys, "seq", axis=1, tiled=True),
        lax.all_gather(cache_values, "seq", axis=1, tiled=True),
    )
    new_keys, new_values = side_by_side((stretch_keys, stretch_values), "seq", 1, 0)
    old_count = old_keys.shape[1]
    new_count = new_keys.shape[1]
    states = absorb(
        states,
        old_keys,
        old_values,
        jnp.arange(old_count, dtype=jnp.int32),
        jnp.ones((old_count,), bool),
    )
    states = absorb(
        states,
        new_keys,
        new_values,
        jnp.arange(new_count, dtype=jnp.int32),
        jnp.zeros((new_count,), bool),
    )
    outputs = [
        (state[2] / state[1][..., None])
        .reshape(seqs, state[2].shape[1], HQ * DH)
        .astype(jnp.bfloat16)
        for state in states
    ]
    attention = outputs[0]
    page_index = own_index * (pre_rows // PAGE) + jnp.arange(pre_rows // PAGE, dtype=jnp.int32)
    prefix_live = page_index[None, :] * PAGE < prefix_len[:, None]
    stretch_live = jnp.ones((seqs, ch_rows // PAGE), bool)
    return (
        attention,
        page_bounds(cache_keys, prefix_live),
        page_bounds(stretch_keys, stretch_live),
    )


def solution(mesh):
    return jax.shard_map(
        on_device,
        mesh=mesh,
        in_specs=(
            P("grp", "seq", None),
            P("grp", "seq", None),
            P("grp", "seq", None),
            P("grp", "seq", None),
            P("grp", "seq", None),
            P("grp"),
        ),
        out_specs=(P("grp", "seq", None), P("grp", "seq", None), P("grp", "seq", None)),
        check_vma=False,
    )
```

profile of v0, /device:TPU:7, one launch (start us, length us, event | category | flops | bytes accessed | tf_op | source)
XLA Modules:
  0.0 371.8 jit_solution(16476472488334940459)
XLA Ops:
  8.7 1.7 pad_maximum_fusion
  10.4 1.5 copy.34
  13.3 1.4 reduce_max.66
  17.0 96.7 %all-gather.4.cloned.1.call-done = bf16[2,2048,1024]{2,1,0:T(8,128)(2,1)} async-done(((bf16[2,64,1024]{2,1,0:T(8,128)(2,1)}), bf16[2,2048,1024]{2,1,0:T(8,128)(2,1)}) %all-gather.4.cloned.1.call-update) | async-done | bytes 8388624 | tf_op jit(solution)/shard_map/all_gather | solution.py:116
  113.7 8.8 %copy.33 = bf16[512,8,8,128]{3,2,1,0:T(8,128)(2,1)} copy(bf16[512,8,8,128]{3,1,2,0:T(8,128)(2,1)} %bitcast.116) | data formatting | bytes 16777216
  122.4 8.9 %copy.19 = bf16[4,2,512,8,128]{4,2,3,1,0:T(8,128)(2,1)} copy(bf16[4,2,512,8,128]{4,3,2,0,1:T(8,128)(2,1)} %bitcast.110) | data formatting | bytes 16777216 | tf_op jit(solution)/shard_map/while | solution.py:77
  131.4 83.1 %all-gather.6.cloned.1.call-done = bf16[2,2048,1024]{2,1,0:T(8,128)(2,1)} async-done(((bf16[2,64,1024]{2,1,0:T(8,128)(2,1)}), bf16[2,2048,1024]{2,1,0:T(8,128)(2,1)}) %all-gather.6.cloned.1.call-update) | async-done | bytes 8388624 | tf_op jit(solution)/shard_map/all_gather | solution.py:117
  214.4 8.8 %copy.35 = bf16[512,8,8,128]{3,2,1,0:T(8,128)(2,1)} copy(bf16[512,8,8,128]{3,1,2,0:T(8,128)(2,1)} %bitcast.117) | data formatting | bytes 16777216
  223.2 8.9 %copy.21 = bf16[4,2,512,8,128]{4,2,3,1,0:T(8,128)(2,1)} copy(bf16[4,2,512,8,128]{4,3,2,0,1:T(8,128)(2,1)} %bitcast.111) | data formatting | bytes 16777216 | tf_op jit(solution)/shard_map/while | solution.py:77
  232.9 71.0 %while.32 = (s32[]{:T(128)}, f32[2,32,8,8]{1,3,2,0:T(8,128)S(1)}, f32[2,32,8,8]{1,3,2,0:T(8,128)}, f32[2,32,8,8,128]{4,3,1,2,0:T(8,128)S(1)}, s32[4,512]{1,0:T(4...) while((s32[]{:T(128)}, f32[2,32,8,8]{1,3,2,0:T(8,128)S(1)}, ...), condition=%wide.region_7.8_spmd, body=%wide.region_1.7_spmd.sunk | while | flops 1091577856 | bytes 34894080 | solution.py:77
  234.8 15.8 %conditional.5 = ((f32[2,32,8,8]{1,3,2,0:T(8,128)S(1)}, f32[2,32,8,8]{1,3,2,0:T(8,128)}, f32[2,32,8,8,128]{4,3,1,2,0:T(8,128)S(1)})) conditional(s32[]{:T(128)} %convert_element_type.34, (f32[2,32,8,8]{1,3,2,0:T(8,128)S(1)}, f32[2,32,8,8]{1,3,2,0:T(8,128)}, f32[2,32,8,8,128]{4,3,1,2,0:T(8,128)S(1)}) %tuple.90, (s32[512]{0:T(512)S(1)}, s32[2]{0:T(128)}, ...), branch_computations={%region_3.3_spmd, %region_4.6_spmd} | conditional | flops 1091576832 | bytes 34887720 | solution.py:75
  235.6 3.0 fusion.2
  238.6 3.6 fusion.5
  242.2 1.5 multiply_add_fusion
  244.7 6.0 %bitcast_add_fusion = f32[2,32,8,8,128]{4,3,1,2,0:T(8,128)S(1)} fusion(f32[2,32,8,8,128]{4,3,1,2,0:T(8,128)S(1)} %get-tuple-element.326, bf16[4,2,512,8,128]{4,2,3,1,0:T(8,128)(2,1)} %get-tuple-element.327, s32[]{:T(128)} %get-tuple-element.323, bf16[2,32,8,8,512]{4,1,3,2,0:T(8,128)(2,1)} %get-tuple-element.502, f32[2,32,8,8]{3,1,2,0:T(8,128)S(1)} %copy.15), kind=kOutput, calls=%fused_computation.13 | convolution fusion | flops 537919488 | bytes 10502656 | tf_op jit(solution)/shard_map/while/body/eval_jaxpr/cond/branch_1_fun/srhgk,skhd->srhgd/dot_general | solution.py:66
  250.7 1.3 compare_reduce_fusion.4
  252.6 15.8 %conditional.5 = ((f32[2,32,8,8]{1,3,2,0:T(8,128)S(1)}, f32[2,32,8,8]{1,3,2,0:T(8,128)}, f32[2,32,8,8,128]{4,3,1,2,0:T(8,128)S(1)})) conditional(s32[]{:T(128)} %convert_element_type.34, (f32[2,32,8,8]{1,3,2,0:T(8,128)S(1)}, f32[2,32,8,8]{1,3,2,0:T(8,128)}, f32[2,32,8,8,128]{4,3,1,2,0:T(8,128)S(1)}) %tuple.90, (s32[512]{0:T(512)S(1)}, s32[2]{0:T(128)}, ...), branch_computations={%region_3.3_spmd, %region_4.6_spmd} | conditional | flops 1091576832 | bytes 34887720 | solution.py:75
  253.3 3.0 fusion.2
  256.3 3.6 fusion.5
  259.9 1.5 multiply_add_fusion
  262.4 5.9 %bitcast_add_fusion = f32[2,32,8,8,128]{4,3,1,2,0:T(8,128)S(1)} fusion(f32[2,32,8,8,128]{4,3,1,2,0:T(8,128)S(1)} %get-tuple-element.326, bf16[4,2,512,8,128]{4,2,3,1,0:T(8,128)(2,1)} %get-tuple-element.327, s32[]{:T(128)} %get-tuple-element.323, bf16[2,32,8,8,512]{4,1,3,2,0:T(8,128)(2,1)} %get-tuple-element.502, f32[2,32,8,8]{3,1,2,0:T(8,128)S(1)} %copy.15), kind=kOutput, calls=%fused_computation.13 | convolution fusion | flops 537919488 | bytes 10502656 | tf_op jit(solution)/shard_map/while/body/eval_jaxpr/cond/branch_1_fun/srhgk,skhd->srhgd/dot_general | solution.py:66
  268.4 1.3 compare_reduce_fusion.4
  270.3 15.8 %conditional.5 = ((f32[2,32,8,8]{1,3,2,0:T(8,128)S(1)}, f32[2,32,8,8]{1,3,2,0:T(8,128)}, f32[2,32,8,8,128]{4,3,1,2,0:T(8,128)S(1)})) conditional(s32[]{:T(128)} %convert_element_type.34, (f32[2,32,8,8]{1,3,2,0:T(8,128)S(1)}, f32[2,32,8,8]{1,3,2,0:T(8,128)}, f32[2,32,8,8,128]{4,3,1,2,0:T(8,128)S(1)}) %tuple.90, (s32[512]{0:T(512)S(1)}, s32[2]{0:T(128)}, ...), branch_computations={%region_3.3_spmd, %region_4.6_spmd} | conditional | flops 1091576832 | bytes 34887720 | solution.py:75
  271.0 3.0 fusion.2
  274.0 3.6 fusion.5
  277.7 1.5 multiply_add_fusion
  280.1 5.9 %bitcast_add_fusion = f32[2,32,8,8,128]{4,3,1,2,0:T(8,128)S(1)} fusion(f32[2,32,8,8,128]{4,3,1,2,0:T(8,128)S(1)} %get-tuple-element.326, bf16[4,2,512,8,128]{4,2,3,1,0:T(8,128)(2,1)} %get-tuple-element.327, s32[]{:T(128)} %get-tuple-element.323, bf16[2,32,8,8,512]{4,1,3,2,0:T(8,128)(2,1)} %get-tuple-element.502, f32[2,32,8,8]{3,1,2,0:T(8,128)S(1)} %copy.15), kind=kOutput, calls=%fused_computation.13 | convolution fusion | flops 537919488 | bytes 10502656 | tf_op jit(solution)/shard_map/while/body/eval_jaxpr/cond/branch_1_fun/srhgk,skhd->srhgd/dot_general | solution.py:66
  288.0 15.9 %conditional.5 = ((f32[2,32,8,8]{1,3,2,0:T(8,128)S(1)}, f32[2,32,8,8]{1,3,2,0:T(8,128)}, f32[2,32,8,8,128]{4,3,1,2,0:T(8,128)S(1)})) conditional(s32[]{:T(128)} %convert_element_type.34, (f32[2,32,8,8]{1,3,2,0:T(8,128)S(1)}, f32[2,32,8,8]{1,3,2,0:T(8,128)}, f32[2,32,8,8,128]{4,3,1,2,0:T(8,128)S(1)}) %tuple.90, (s32[512]{0:T(512)S(1)}, s32[2]{0:T(128)}, ...), branch_computations={%region_3.3_spmd, %region_4.6_spmd} | conditional | flops 1091576832 | bytes 34887720 | solution.py:75
  288.8 3.0 fusion.2
  291.8 3.6 fusion.5
  295.4 1.5 multiply_add_fusion
  297.9 6.0 %bitcast_add_fusion = f32[2,32,8,8,128]{4,3,1,2,0:T(8,128)S(1)} fusion(f32[2,32,8,8,128]{4,3,1,2,0:T(8,128)S(1)} %get-tuple-element.326, bf16[4,2,512,8,128]{4,2,3,1,0:T(8,128)(2,1)} %get-tuple-element.327, s32[]{:T(128)} %get-tuple-element.323, bf16[2,32,8,8,512]{4,1,3,2,0:T(8,128)(2,1)} %get-tuple-element.502, f32[2,32,8,8]{3,1,2,0:T(8,128)S(1)} %copy.15), kind=kOutput, calls=%fused_computation.13 | convolution fusion | flops 537919488 | bytes 10502656 | tf_op jit(solution)/shard_map/while/body/eval_jaxpr/cond/branch_1_fun/srhgk,skhd->srhgd/dot_general | solution.py:66
  303.9 11.9 %all-gather.8.cloned.1.call-done = bf16[4,1024,1024]{2,1,0:T(8,128)(2,1)} async-done(((bf16[4,32,1024]{2,1,0:T(8,128)(2,1)}), bf16[4,1024,1024]{2,1,0:T(8,128)(2,1)}) %all-gather.8.cloned.1.call-update) | async-done | bytes 8388624 | tf_op jit(solution)/shard_map/all_gather | solution.py:16
  315.9 3.9 %fusion.38 = (bf16[2,1024,1024]{2,1,0:T(8,128)(2,1)S(1)}, bf16[2,1024,1024]{2,1,0:T(8,128)(2,1)S(1)}) fusion(bf16[4,1024,1024]{2,1,0:T(8,128)(2,1)} %all-gather.8.cloned.1.call-done), kind=kLoop, calls=%fused_computation.59 | loop fusion | bytes 16777216 | tf_op jit(solution)/shard_map/slice | solution.py:18
  320.9 2.9 copy.22
  324.9 2.9 copy.24
  327.8 34.3 %while.33 = (s32[]{:T(128)}, f32[2,32,8,8]{1,3,2,0:T(8,128)S(1)}, f32[2,32,8,8]{1,3,2,0:T(8,128)}, f32[2,32,8,8,128]{4,3,1,2,0:T(8,128)S(1)}, s32[2,512]{1,0:T(2...) while((s32[]{:T(128)}, f32[2,32,8,8]{1,3,2,0:T(8,128)S(1)}, ...), condition=%wide.region_15.16_spmd.clone, body=%wide.region_9.15_spmd.clone.sunk | while | flops 1091593216 | bytes 34940688 | solution.py:77
  329.7 15.2 %conditional.6 = ((f32[2,32,8,8]{1,3,2,0:T(8,128)S(1)}, f32[2,32,8,8]{1,3,2,0:T(8,128)}, f32[2,32,8,8,128]{4,3,1,2,0:T(8,128)S(1)})) conditional(s32[]{:T(128)} %convert_element_type.35, (f32[2,32,8,8]{1,3,2,0:T(8,128)S(1)}, f32[2,32,8,8]{1,3,2,0:T(8,128)}, f32[2,32,8,8,128]{4,3,1,2,0:T(8,128)S(1)}) %tuple.93, (s32[512]{0:T(512)S(1)}, ...), branch_computations={%region_11.11_spmd, %region_12.14_spmd.clone} | conditional | flops 1091592192 | bytes 34934180 | solution.py:75
  329.8 3.0 fusion.20
  332.8 3.7 fusion.23
  336.5 1.5 multiply_add_fusion.1
  338.9 5.9 %bitcast_add_fusion.1 = f32[2,32,8,8,128]{4,3,1,2,0:T(8,128)S(1)} fusion(f32[2,32,8,8,128]{4,3,1,2,0:T(8,128)S(1)} %get-tuple-element.438, bf16[2,2,512,8,128]{4,2,3,1,0:T(8,128)(2,1)} %get-tuple-element.439, s32[]{:T(128)} %get-tuple-element.435, bf16[2,32,8,8,512]{4,1,3,2,0:T(8,128)(2,1)} %get-tuple-element.506, f32[2,32,8,8]{3,1,2,0:T(8,128)S(1)} %copy.31), kind=kOutput, calls=%fused_computation.35 | convolution fusion | flops 537919488 | bytes 10502656 | tf_op jit(solution)/shard_map/while/body/eval_jaxpr/cond/branch_1_fun/srhgk,skhd->srhgd/dot_general | solution.py:66
  346.8 15.2 %conditional.6 = ((f32[2,32,8,8]{1,3,2,0:T(8,128)S(1)}, f32[2,32,8,8]{1,3,2,0:T(8,128)}, f32[2,32,8,8,128]{4,3,1,2,0:T(8,128)S(1)})) conditional(s32[]{:T(128)} %convert_element_type.35, (f32[2,32,8,8]{1,3,2,0:T(8,128)S(1)}, f32[2,32,8,8]{1,3,2,0:T(8,128)}, f32[2,32,8,8,128]{4,3,1,2,0:T(8,128)S(1)}) %tuple.93, (s32[512]{0:T(512)S(1)}, ...), branch_computations={%region_11.11_spmd, %region_12.14_spmd.clone} | conditional | flops 1091592192 | bytes 34934180 | solution.py:75
  346.9 3.0 fusion.20
  349.9 3.7 fusion.23
  353.6 1.5 multiply_add_fusion.1
  356.1 5.9 %bitcast_add_fusion.1 = f32[2,32,8,8,128]{4,3,1,2,0:T(8,128)S(1)} fusion(f32[2,32,8,8,128]{4,3,1,2,0:T(8,128)S(1)} %get-tuple-element.438, bf16[2,2,512,8,128]{4,2,3,1,0:T(8,128)(2,1)} %get-tuple-element.439, s32[]{:T(128)} %get-tuple-element.435, bf16[2,32,8,8,512]{4,1,3,2,0:T(8,128)(2,1)} %get-tuple-element.506, f32[2,32,8,8]{3,1,2,0:T(8,128)S(1)} %copy.31), kind=kOutput, calls=%fused_computation.35 | convolution fusion | flops 537919488 | bytes 10502656 | tf_op jit(solution)/shard_map/while/body/eval_jaxpr/cond/branch_1_fun/srhgk,skhd->srhgd/dot_general | solution.py:66
  364.0 1.3 convert_element_type.26
  (66 shorter events, 24.1 us)
Async XLA Ops:
  7.2 7.6 %copy-start = (bf16[2,64,1024]{2,1,0:T(8,128)(2,1)S(1)}, bf16[2,64,1024]{2,1,0:T(8,128)(2,1)}, u32[]{:S(2)}) copy-start(bf16[2,64,1024]{2,1,0:T(8,128)(2,1)} %param.17) | copy-start | bytes 786436
  7.2 7.5 %copy-start.1 = (bf16[2,32,1024]{2,1,0:T(8,128)(2,1)S(1)}, bf16[2,32,1024]{2,1,0:T(8,128)(2,1)}, u32[]{:S(2)}) copy-start(bf16[2,32,1024]{2,1,0:T(8,128)(2,1)} %param.15) | copy-start | bytes 393220
  7.2 106.5 %all-gather.4.cloned.1.call-start = ((), (), s32[]{:S(2)}) async-start(), calls=%async_computation | async-start | bytes 8650752 | tf_op jit(solution)/shard_map/all_gather | solution.py:116
  7.9 206.5 %all-gather.6.cloned.1.call-start = ((), (), s32[]{:S(2)}) async-start(), calls=%async_computation.1 | async-start | bytes 8650752 | tf_op jit(solution)/shard_map/all_gather | solution.py:117
  8.7 307.2 %all-gather.8.cloned.1.call-start = ((), (), s32[]{:S(2)}) async-start(), calls=%async_computation.2 | async-start | bytes 8650752 | tf_op jit(solution)/shard_map/all_gather | solution.py:16
Sparse Core Ops, SparseCore 0:
  10.8 102.8 all-gather.3
  116.5 97.8 all-gather.5
  217.8 98.0 all-gather.7
where the time goes:
time: 373 us; the launch traced here: 372 us
  waiting for transfers between devices  193 us (52%)
  local copies, waits for them, and re-layouts  58.6 us (16%)
  matrix products  53.5 us (14%)
  other arithmetic  48.3 us (13%)
  between operations  13.9 us (4%)
  loops' own time  4.3 us (1%)
    all_gather x1, waiting for transfers between devices, on_device(): lax.all_gather(cache_keys, 'seq', axis=1, tiled=True)  96.7 us
    all_gather x1, waiting for transfers between devices, on_device(): lax.all_gather(cache_values, 'seq', axis=1, tiled=True)  83.1 us
    dot_general x6, matrix products, compute(): jnp.einsum('srhgk,skhd->srhgd', weights.astype(jnp.bfloat16), value_part,...  35.7 us
    unnamed x11, local copies, waits for them, and re-layouts  26.9 us
    convert_element_type x6, other arithmetic, compute(): weights.astype(jnp.bfloat16)  21.9 us
    while x4, local copies, waits for them, and re-layouts, online(): lax.scan(one_step, state, (key_blocks, value_blocks, pos_blocks, cache_bl...  19.5 us
    dot_general x6, matrix products, compute(): jnp.einsum('srhgd,skhd->srhgk', shaped_query, key_part, preferred_element...  17.8 us
    all_gather x1, waiting for transfers between devices, side_by_side(): lax.all_gather(both, axis, axis=dim, tiled=True)  11.9 us
  transfers between devices with their start and end apart: 3, of which 3 were waited for; matrix products, arithmetic and copies ran while one was open for 30% of the time, Pallas kernels for 0%

commit v1 on v0

v1 whole, which is shorter than its diff:
```python
import functools
import math

import jax
import jax.numpy as jnp
from jax import lax
from jax.experimental import pallas as pl
from jax.experimental.pallas import tpu as pltpu
from jax.sharding import PartitionSpec as P

MESH = pl.DeviceIdType.MESH
DH = 128
PAGE = 16
GROUP = 8
WIDTH = GROUP * DH
NZ = 8
NX = 2
OWNERS = NX * NZ
CHUNK = 256
DEAD = -1e30
FACTOR = math.log2(math.e) / math.sqrt(DH)


def offset_of(k):
    t = k // 2
    half = (t + 1) // 2
    return k % 2, half * (1 - 2 * ((t + 1) % 2))


def kernel(
    plen_ref, q_hbm, sk_hbm, sv_hbm, ck_hbm, cv_hbm,
    out_hbm, pb_ref, sb_ref,
    q_st, c_st, s_st, q_in, c_in, s_in, o_st, scores,
    load_sem, c_send, c_recv, s_send, s_recv, q_send, q_recv, o_send, o_recv,
    fc_send, fc_recv, fs_send, fs_recv, own_sem,
):
    grp = lax.axis_index("grp")
    seq = lax.axis_index("seq")
    x, z, core = seq // (2 * NZ), (seq // 2) % NZ, seq % 2
    rows = q_hbm.shape[1]
    pre_rows = ck_hbm.shape[1]

    def place(px, pz, pc):
        return (px % NX) * (2 * NZ) + ((pz + NZ) % NZ) * 2 + pc

    def target(k):
        dx, dz = offset_of(k)
        return (x + dx) % NX, (z + dz + NZ) % NZ

    def origin(k):
        dx, dz = offset_of(k)
        return (x + dx) % NX, (z - dz + NZ) % NZ

    loads = [
        pltpu.make_async_copy(ck_hbm, c_st.at[:, 0], load_sem.at[0]),
        pltpu.make_async_copy(cv_hbm, c_st.at[:, 1], load_sem.at[1]),
        pltpu.make_async_copy(sk_hbm, s_st.at[:, 0], load_sem.at[2]),
        pltpu.make_async_copy(sv_hbm, s_st.at[:, 1], load_sem.at[3]),
        pltpu.make_async_copy(q_hbm, q_st, load_sem.at[4]),
    ]
    for copy in loads:
        copy.start()

    barrier = pltpu.get_barrier_semaphore()
    for k in range(1, OWNERS):
        tx, tz = target(k)
        pl.semaphore_signal(
            barrier, inc=1, device_id=(grp, place(tx, tz, core)), device_id_type=MESH
        )
    partner = (grp, place(x, z, 1 - core))
    pl.semaphore_signal(barrier, inc=1, device_id=partner, device_id_type=MESH)
    for copy in loads:
        copy.wait()
    pl.semaphore_wait(barrier, OWNERS)

    def cols(g, width):
        return pl.ds(pl.multiple_of(g * width, width), width)

    def c_rows(i):
        return pl.ds(pl.multiple_of(i * pre_rows, pre_rows), pre_rows)

    def s_rows(i):
        return pl.ds(pl.multiple_of(i * rows, rows), rows)

    def c_copy(k):
        tx, tz = target(k)
        return pltpu.make_async_remote_copy(
            src_ref=c_st.at[tx, :, :, cols(tz, DH)], dst_ref=c_in.at[:, c_rows(seq)],
            send_sem=c_send.at[k], recv_sem=c_recv.at[k],
            device_id=(grp, place(tx, tz, core)), device_id_type=MESH,
        )

    def s_copy(k):
        tx, tz = target(k)
        return pltpu.make_async_remote_copy(
            src_ref=s_st.at[tx, :, :, cols(tz, DH)], dst_ref=s_in.at[:, s_rows(seq)],
            send_sem=s_send.at[k], recv_sem=s_recv.at[k],
            device_id=(grp, place(tx, tz, core)), device_id_type=MESH,
        )

    def q_copy(k):
        tx, tz = target(k)
        return pltpu.make_async_remote_copy(
            src_ref=q_st.at[tx, :, cols(tz, WIDTH)], dst_ref=q_in.at[k],
            send_sem=q_send.at[k], recv_sem=q_recv.at[k],
            device_id=(grp, place(tx, tz, core)), device_id_type=MESH,
        )

    def o_copy(k):
        ox, oz = origin(k)
        return pltpu.make_async_remote_copy(
            src_ref=o_st.at[k], dst_ref=out_hbm.at[x, :, cols(z, WIDTH)],
            send_sem=o_send.at[k], recv_sem=o_recv.at[k],
            device_id=(grp, place(ox, oz, core)), device_id_type=MESH,
        )

    def forward(k):
        ox, oz = origin(k)
        i = place(ox, oz, core)
        return (
            pltpu.make_async_remote_copy(
                src_ref=c_in.at[:, c_rows(i)], dst_ref=c_in.at[:, c_rows(i)],
                send_sem=fc_send.at[k], recv_sem=fc_recv.at[k],
                device_id=partner, device_id_type=MESH,
            ),
            pltpu.make_async_remote_copy(
                src_ref=s_in.at[:, s_rows(i)], dst_ref=s_in.at[:, s_rows(i)],
                send_sem=fs_send.at[k], recv_sem=fs_recv.at[k],
                device_id=partner, device_id_type=MESH,
            ),
        )

    for k in range(1, OWNERS):
        c_copy(k).start()
        s_copy(k).start()
    for k in range(1, OWNERS):
        q_copy(k).start()

    own = [
        pltpu.make_async_copy(c_st.at[x, :, :, cols(z, DH)], c_in.at[:, c_rows(seq)], own_sem.at[0]),
        pltpu.make_async_copy(s_st.at[x, :, :, cols(z, DH)], s_in.at[:, s_rows(seq)], own_sem.at[1]),
        pltpu.make_async_copy(q_st.at[x, :, cols(z, WIDTH)], q_in.at[0], own_sem.at[2]),
    ]
    for copy in own:
        copy.start()

    page0 = seq * (pre_rows // PAGE)

    def bounds(held, s, pages):
        lows, highs = [], []
        for p in range(pages):
            page = held[s, 0, p * PAGE:(p + 1) * PAGE, :].astype(jnp.float32)
            lows.append(jnp.min(page, axis=0, keepdims=True))
            highs.append(jnp.max(page, axis=0, keepdims=True))
        return jnp.concatenate(
            [jnp.concatenate(lows, axis=0), jnp.concatenate(highs, axis=0)], axis=1
        )

    for s in range(c_st.shape[0]):
        pages = pre_rows // PAGE
        both = bounds(c_st, s, pages)
        page = page0 + lax.broadcasted_iota(jnp.int32, both.shape, 0)
        pb_ref[s] = jnp.where(page * PAGE < plen_ref[s], both, 0.0).astype(jnp.bfloat16)
        sb_ref[s] = bounds(s_st, s, rows // PAGE).astype(jnp.bfloat16)

    for copy in own:
        copy.wait()
    for k in range(OWNERS):
        if k:
            c_copy(k).wait_recv()
            s_copy(k).wait_recv()
        for copy in forward(k):
            copy.start()
    for k in range(OWNERS):
        for copy in forward(k):
            copy.wait_recv()

    length = plen_ref[x]
    block_rows = GROUP * rows
    n_pre = c_in.shape[1] // CHUNK
    n_new = s_in.shape[1] // CHUNK

    def attend(k):
        ox, oz = origin(k)
        first = place(ox, oz, core) * rows
        q = jnp.concatenate([q_in[k, :, h * DH:(h + 1) * DH] for h in range(GROUP)], axis=0)
        lane = lax.broadcasted_iota(jnp.int32, (1, CHUNK), 1)
        row = first + lax.broadcasted_iota(jnp.int32, (block_rows, 1), 0) % rows
        top = jnp.full((block_rows, DH), DEAD, jnp.float32)
        for j in range(n_pre + n_new):
            if j < n_pre:
                key = c_in[0, j * CHUNK:(j + 1) * CHUNK, :]
                live = lane + j * CHUNK < length
            else:
                key = s_in[0, (j - n_pre) * CHUNK:(j - n_pre + 1) * CHUNK, :]
                live = lane + (j - n_pre) * CHUNK <= row
            s = lax.dot_general(
                q, key, (((1,), (1,)), ((), ())), preferred_element_type=jnp.float32
            )
            s = jnp.where(live, s, DEAD)
            scores[:, j * CHUNK:(j + 1) * CHUNK] = s
            for i in range(CHUNK // DH):
                top = jnp.maximum(top, s[:, i * DH:(i + 1) * DH])
        top = jnp.max(top, axis=1, keepdims=True)
        total = jnp.zeros((block_rows, DH), jnp.float32)
        acc = jnp.zeros((block_rows, DH), jnp.float32)
        for j in range(n_pre + n_new):
            if j < n_pre:
                value = c_in[1, j * CHUNK:(j + 1) * CHUNK, :]
            else:
                value = s_in[1, (j - n_pre) * CHUNK:(j - n_pre + 1) * CHUNK, :]
            w = jnp.exp2((scores[:, j * CHUNK:(j + 1) * CHUNK] - top) * FACTOR)
            for i in range(CHUNK // DH):
                total = total + w[:, i * DH:(i + 1) * DH]
            acc = acc + jnp.dot(
                w.astype(jnp.bfloat16), value, preferred_element_type=jnp.float32
            )
        out = (acc / jnp.sum(total, axis=1, keepdims=True)).astype(jnp.bfloat16)
        for h in range(GROUP):
            o_st[k, :, h * DH:(h + 1) * DH] = out[h * rows:(h + 1) * rows, :]

    def step(k, carry):
        q_copy(k).wait_recv()
        attend(k)

        @pl.when(k > 1)
        def _():
            o_copy(k - 1).start()

        return carry

    lax.fori_loop(1, OWNERS, step, 0)
    o_copy(OWNERS - 1).start()
    attend(0)
    mine = pltpu.make_async_copy(o_st.at[0], out_hbm.at[x, :, cols(z, WIDTH)], own_sem.at[0])
    mine.start()

    for k in range(1, OWNERS):
        c_copy(k).wait_send()
        s_copy(k).wait_send()
        q_copy(k).wait_send()
    for k in range(OWNERS):
        for copy in forward(k):
            copy.wait_send()
    for k in range(1, OWNERS):
        o_copy(k).wait()
    mine.wait()


def on_device(queries, stretch_keys, stretch_values, cache_keys, cache_values, prefix_len):
    seqs, rows, wide = queries.shape
    pre_rows, width = cache_keys.shape[1:]
    members = lax.axis_size("seq")
    dma = pltpu.SemaphoreType.DMA
    any_spec = pl.BlockSpec(memory_space=pl.ANY)
    vmem_spec = pl.BlockSpec(memory_space=pltpu.VMEM)
    attention, pb, sb = pl.pallas_call(
        kernel,
        out_shape=(
            jax.ShapeDtypeStruct((seqs, rows, wide), jnp.bfloat16),
            jax.ShapeDtypeStruct((seqs, pre_rows // PAGE, 2 * width), jnp.bfloat16),
            jax.ShapeDtypeStruct((seqs, rows // PAGE, 2 * width), jnp.bfloat16),
        ),
        in_specs=[pl.BlockSpec(memory_space=pltpu.SMEM)] + [any_spec] * 5,
        out_specs=(any_spec, vmem_spec, vmem_spec),
        scratch_shapes=[
            pltpu.VMEM((seqs, rows, wide), jnp.bfloat16),
            pltpu.VMEM((seqs, 2, pre_rows, width), jnp.bfloat16),
            pltpu.VMEM((seqs, 2, rows, width), jnp.bfloat16),
            pltpu.VMEM((OWNERS, rows, WIDTH), jnp.bfloat16),
            pltpu.VMEM((2, members * pre_rows, DH), jnp.bfloat16),
            pltpu.VMEM((2, members * rows, DH), jnp.bfloat16),
            pltpu.VMEM((OWNERS, rows, WIDTH), jnp.bfloat16),
            pltpu.VMEM((GROUP * rows, members * (pre_rows + rows)), jnp.float32),
            dma((5,)),
        ]
        + [dma((OWNERS,))] * 12
        + [dma((3,))],
        compiler_params=pltpu.CompilerParams(
            collective_id=0, has_side_effects=True, vmem_limit_bytes=56 * 2**20
        ),
        name="attend",
    )(prefix_len, queries, stretch_keys, stretch_values, cache_keys, cache_values)
    return attention, pb, sb


def solution(mesh):
    spec = P("grp", "seq", None)
    return jax.shard_map(
        on_device,
        mesh=mesh,
        in_specs=(spec, spec, spec, spec, spec, P("grp")),
        out_specs=(spec, spec, spec),
        check_vma=False,
    )
```

time: 373 us -> 80.5 us (0.22)
  the two profiles are of different devices: /device:TPU:7 before, /device:TPU:8 now
where the time goes in v1:
time: 80.5 us; the launch traced here: 79 us
  Pallas kernels  74.8 us (93%)
  local copies, waits for them, and re-layouts  3.61 us (4%)
    pallas_call x1, Pallas kernels, on_device(): pl.pallas_call(kernel, out_shape=(jax.ShapeDtypeStruct((seqs, rows, wide)...  74.8 us
    unnamed x7, local copies, waits for them, and re-layouts  3.61 us

profile of v1, /device:TPU:8, one launch (start us, length us, event | category | flops | bytes accessed | tf_op | source)
XLA Modules:
  0.0 79.0 jit_solution(9184113011275818640)
XLA Ops:
  0.6 74.8 %attend.1 = (bf16[2,32,8192]{2,1,0:T(8,128)(2,1)}, bf16[2,4,2048]{2,1,0:T(4,128)(2,1)}, bf16[2,2,2048]{2,1,0:T(2,128)(2,1)}) custom-call(s32[2]{0:T(128)} %plen_ref.1, bf16[2,32,8192]{2,1,0:T(8,128)(2,1)} %q_hbm.1, bf16[2,32,1024]{2,1,0:T(8,128)(2,1)} %sk_hbm.1, bf16[2,32,1024]{2,1,0:T(8,128)(2,1)} %sv_hbm.1, bf16[2,64,1024]{2,1,0:T(8,128)(2,1)} %ck_hbm.1, ...), custom_call_target="tpu_custom_call" | custom-call | tf_op jit(solution)/shard_map/attend/pallas_call | solution.py:257
  75.4 0.0 copy-start
  75.4 2.3 %copy.12 = bf16[2,32,8192]{2,1,0:T(8,128)(2,1)} copy(bf16[2,32,8192]{2,1,0:T(8,128)(2,1)} %get-tuple-element.6) | data formatting | bytes 2097152
  77.7 0.0 copy-done
  77.7 0.0 copy-start.1
  77.7 0.6 copy.13
  78.3 0.1 copy-done.1
  78.4 0.6 copy.14
Async XLA Ops:
  75.4 2.3 %copy-start = (bf16[2,4,2048]{2,1,0:T(4,128)(2,1)S(1)}, bf16[2,4,2048]{2,1,0:T(4,128)(2,1)}, u32[]{:S(2)}) copy-start(bf16[2,4,2048]{2,1,0:T(4,128)(2,1)} %get-tuple-element.7) | copy-start | bytes 98308
  77.7 0.7 copy-start.1

commit v2 on v1

--- a/solution.py
+++ b/solution.py
@@ -29,10 +29,10 @@
 
 def kernel(
     plen_ref, q_hbm, sk_hbm, sv_hbm, ck_hbm, cv_hbm,
-    out_hbm, pb_ref, sb_ref,
+    out_ref, pb_ref, sb_ref,
     q_st, c_st, s_st, q_in, c_in, s_in, o_st, scores,
     load_sem, c_send, c_recv, s_send, s_recv, q_send, q_recv, o_send, o_recv,
-    fc_send, fc_recv, fs_send, fs_recv, own_sem,
+    fc_send, fc_recv, fs_send, fs_recv, own_sem, chain,
 ):
     grp = lax.axis_index("grp")
     seq = lax.axis_index("seq")
@@ -61,17 +61,20 @@
     for copy in loads:
         copy.start()
 
+    partner = (grp, place(x, z, 1 - core))
+    above, below = (grp, place(x, z + 1, core)), (grp, place(x, z - 1, core))
+    across = (grp, place(x + 1, z, core))
     barrier = pltpu.get_barrier_semaphore()
-    for k in range(1, OWNERS):
-        tx, tz = target(k)
-        pl.semaphore_signal(
-            barrier, inc=1, device_id=(grp, place(tx, tz, core)), device_id_type=MESH
-        )
-    partner = (grp, place(x, z, 1 - core))
-    pl.semaphore_signal(barrier, inc=1, device_id=partner, device_id_type=MESH)
-    for copy in loads:
-        copy.wait()
-    pl.semaphore_wait(barrier, OWNERS)
+    for near in (above, below, across, partner):
+        pl.semaphore_signal(barrier, inc=1, device_id=near, device_id_type=MESH)
+
+    def tell(level):
+        pl.semaphore_signal(chain.at[0, level], inc=1, device_id=above, device_id_type=MESH)
+        pl.semaphore_signal(chain.at[1, level], inc=1, device_id=below, device_id_type=MESH)
+
+    def hear(level):
+        pl.semaphore_wait(chain.at[0, level], 1)
+        pl.semaphore_wait(chain.at[1, level], 1)
 
     def cols(g, width):
         return pl.ds(pl.multiple_of(g * width, width), width)
@@ -109,7 +112,7 @@
     def o_copy(k):
         ox, oz = origin(k)
         return pltpu.make_async_remote_copy(
-            src_ref=o_st.at[k], dst_ref=out_hbm.at[x, :, cols(z, WIDTH)],
+            src_ref=o_st.at[k], dst_ref=out_ref.at[x, :, cols(z, WIDTH)],
             send_sem=o_send.at[k], recv_sem=o_recv.at[k],
             device_id=(grp, place(ox, oz, core)), device_id_type=MESH,
         )
@@ -130,9 +133,28 @@
             ),
         )
 
-    for k in range(1, OWNERS):
-        c_copy(k).start()
-        s_copy(k).start()
+    def give(*partners):
+        for k in partners:
+            c_copy(k).start()
+            s_copy(k).start()
+
+    for copy in loads[:4]:
+        copy.wait()
+    pl.semaphore_wait(barrier, 4)
+    tell(0)
+    give(2, 4, 1)
+    hear(0)
+    tell(1)
+    give(3, 5, 6, 8)
+    hear(1)
+    tell(2)
+    give(7, 9, 10, 12)
+    hear(2)
+    tell(3)
+    give(11, 13, 14)
+    hear(3)
+    give(15)
+    loads[4].wait()
     for k in range(1, OWNERS):
         q_copy(k).start()
 
@@ -232,7 +254,7 @@
     lax.fori_loop(1, OWNERS, step, 0)
     o_copy(OWNERS - 1).start()
     attend(0)
-    mine = pltpu.make_async_copy(o_st.at[0], out_hbm.at[x, :, cols(z, WIDTH)], own_sem.at[0])
+    mine = pltpu.make_async_copy(o_st.at[0], out_ref.at[x, :, cols(z, WIDTH)], own_sem.at[0])
     mine.start()
 
     for k in range(1, OWNERS):
@@ -254,15 +276,16 @@
     dma = pltpu.SemaphoreType.DMA
     any_spec = pl.BlockSpec(memory_space=pl.ANY)
     vmem_spec = pl.BlockSpec(memory_space=pltpu.VMEM)
-    attention, pb, sb = pl.pallas_call(
+    shapes = (
+        (seqs, rows, wide),
+        (seqs, pre_rows // PAGE, 2 * width),
+        (seqs, rows // PAGE, 2 * width),
+    )
+    return pl.pallas_call(
         kernel,
-        out_shape=(
-            jax.ShapeDtypeStruct((seqs, rows, wide), jnp.bfloat16),
-            jax.ShapeDtypeStruct((seqs, pre_rows // PAGE, 2 * width), jnp.bfloat16),
-            jax.ShapeDtypeStruct((seqs, rows // PAGE, 2 * width), jnp.bfloat16),
-        ),
+        out_shape=tuple(pltpu.VMEM(shape, jnp.bfloat16) for shape in shapes),
         in_specs=[pl.BlockSpec(memory_space=pltpu.SMEM)] + [any_spec] * 5,
-        out_specs=(any_spec, vmem_spec, vmem_spec),
+        out_specs=(vmem_spec,) * 3,
         scratch_shapes=[
             pltpu.VMEM((seqs, rows, wide), jnp.bfloat16),
             pltpu.VMEM((seqs, 2, pre_rows, width), jnp.bfloat16),
@@ -275,14 +298,12 @@
             dma((5,)),
         ]
         + [dma((OWNERS,))] * 12
-        + [dma((3,))],
+        + [dma((3,)), pltpu.SemaphoreType.REGULAR((2, NZ // 2))],
         compiler_params=pltpu.CompilerParams(
             collective_id=0, has_side_effects=True, vmem_limit_bytes=56 * 2**20
         ),
         name="attend",
     )(prefix_len, queries, stretch_keys, stretch_values, cache_keys, cache_values)
-    return attention, pb, sb
-
 
 def solution(mesh):
     spec = P("grp", "seq", None)

time: 80.5 us -> 78.2 us (0.971)
  local copies, waits for them, and re-layouts: 3.61 us -> 2.19 us
  Pallas kernels: 74.8 us -> 73.8 us
    unnamed x7 -> x3, local copies, waits for them, and re-layouts: 3.61 us -> 2.19 us
    pallas_call x1, Pallas kernels: 74.8 us -> 73.8 us  [on_device(): pl.pallas_call(kernel, out_shape=tuple((pltpu.VMEM(shape, jnp.bfloat16) f...]
where the time goes in v2:
time: 78.2 us; the launch traced here: 76.6 us
  Pallas kernels  73.8 us (94%)
  local copies, waits for them, and re-layouts  2.19 us (3%)
    pallas_call x1, Pallas kernels, on_device(): pl.pallas_call(kernel, out_shape=tuple((pltpu.VMEM(shape, jnp.bfloat16) f...  73.8 us
    unnamed x3, local copies, waits for them, and re-layouts  2.19 us

profile of v2, /device:TPU:8, one launch (start us, length us, event | category | flops | bytes accessed | tf_op | source)
XLA Modules:
  0.0 76.6 jit_solution(17668883919145347682)
XLA Ops:
  0.6 73.8 %attend.1 = (bf16[2,32,8192]{2,1,0:T(8,128)(2,1)S(1)}, bf16[2,4,2048]{2,1,0:T(4,128)(2,1)S(1)}, bf16[2,2,2048]{2,1,0:T(2,128)(2,1)S(1)}) custom-call(s32[2]{0:T(128)} %plen_ref.1, bf16[2,32,8192]{2,1,0:T(8,128)(2,1)} %q_hbm.1, bf16[2,32,1024]{2,1,0:T(8,128)(2,1)} %sk_hbm.1, bf16[2,32,1024]{2,1,0:T(8,128)(2,1)} %sv_hbm.1, bf16[2,64,1024]{2,1,0:T(8,128)(2,1)} %ck_hbm.1, ...), custom_call_target="tpu_custom_call" | custom-call | tf_op jit(solution)/shard_map/attend/pallas_call | solution.py:284
  74.4 1.0 %copy.12 = bf16[2,32,8192]{2,1,0:T(8,128)(2,1)} copy(bf16[2,32,8192]{2,1,0:T(8,128)(2,1)S(1)} %get-tuple-element.3) | data formatting | bytes 2097152
  75.4 0.6 copy.14
  76.0 0.6 copy.13

commit v3 on v2

--- a/solution.py
+++ b/solution.py
@@ -155,7 +155,7 @@
     hear(3)
     give(15)
     loads[4].wait()
-    for k in range(1, OWNERS):
+    for k in reversed(range(1, OWNERS)):
         q_copy(k).start()
 
     own = [
@@ -241,18 +241,19 @@
         for h in range(GROUP):
             o_st[k, :, h * DH:(h + 1) * DH] = out[h * rows:(h + 1) * rows, :]
 
-    def step(k, carry):
+    def step(i, carry):
+        k = OWNERS - 1 - i
         q_copy(k).wait_recv()
         attend(k)
 
-        @pl.when(k > 1)
+        @pl.when(i > 0)
         def _():
-            o_copy(k - 1).start()
+            o_copy(k + 1).start()
 
         return carry
 
-    lax.fori_loop(1, OWNERS, step, 0)
-    o_copy(OWNERS - 1).start()
+    lax.fori_loop(0, OWNERS - 1, step, 0)
+    o_copy(1).start()
     attend(0)
     mine = pltpu.make_async_copy(o_st.at[0], out_ref.at[x, :, cols(z, WIDTH)], own_sem.at[0])
     mine.start()
@@ -267,6 +268,16 @@
     for k in range(1, OWNERS):
         o_copy(k).wait()
     mine.wait()
+
+
+def put_out(*refs):
+    *ends, sem = refs
+    half = len(ends) // 2
+    copies = [pltpu.make_async_copy(ends[i], ends[half + i], sem.at[i]) for i in range(half)]
+    for copy in copies:
+        copy.start()
+    for copy in copies:
+        copy.wait()
 
 
 def on_device(queries, stretch_keys, stretch_values, cache_keys, cache_values, prefix_len):
@@ -281,7 +292,7 @@
         (seqs, pre_rows // PAGE, 2 * width),
         (seqs, rows // PAGE, 2 * width),
     )
-    return pl.pallas_call(
+    held = pl.pallas_call(
         kernel,
         out_shape=tuple(pltpu.VMEM(shape, jnp.bfloat16) for shape in shapes),
         in_specs=[pl.BlockSpec(memory_space=pltpu.SMEM)] + [any_spec] * 5,
@@ -304,6 +315,15 @@
         ),
         name="attend",
     )(prefix_len, queries, stretch_keys, stretch_values, cache_keys, cache_values)
+    held = [pltpu.with_memory_space_constraint(array, pltpu.VMEM) for array in held]
+    return pl.pallas_call(
+        put_out,
+        out_shape=tuple(jax.ShapeDtypeStruct(shape, jnp.bfloat16) for shape in shapes),
+        in_specs=[vmem_spec] * 3,
+        out_specs=(any_spec,) * 3,
+        scratch_shapes=[dma((3,))],
+        name="put_out",
+    )(*held)
 
 def solution(mesh):
     spec = P("grp", "seq", None)

time: 78.2 us -> 76.2 us (0.974); the launches traced: 76.6 us -> 76.1 us
  local copies, waits for them, and re-layouts: 2.19 us -> 0 us
  Pallas kernels: 73.8 us -> 75.5 us
    unnamed x3 -> x0, local copies, waits for them, and re-layouts: 2.19 us -> none
    pallas_call x0 -> x1, Pallas kernels: none -> 1 us  [on_device(): pl.pallas_call(put_out, out_shape=tuple((jax.ShapeDtypeStruct(shape, jnp....]
where the time goes in v3:
time: 76.2 us; the launch traced here: 76.1 us
  Pallas kernels  75.5 us (99%)
    pallas_call x1, Pallas kernels, on_device(): pl.pallas_call(kernel, out_shape=tuple((pltpu.VMEM(shape, jnp.bfloat16) f...  74.5 us

profile of v3, /device:TPU:8, one launch (start us, length us, event | category | flops | bytes accessed | tf_op | source)
XLA Modules:
  0.0 76.1 jit_solution(2766919322443821586)
XLA Ops:
  0.6 74.5 %attend.1 = (bf16[2,32,8192]{2,1,0:T(8,128)(2,1)S(1)}, bf16[2,4,2048]{2,1,0:T(4,128)(2,1)S(1)}, bf16[2,2,2048]{2,1,0:T(2,128)(2,1)S(1)}) custom-call(s32[2]{0:T(128)} %plen_ref.1, bf16[2,32,8192]{2,1,0:T(8,128)(2,1)} %q_hbm.1, bf16[2,32,1024]{2,1,0:T(8,128)(2,1)} %sk_hbm.1, bf16[2,32,1024]{2,1,0:T(8,128)(2,1)} %sv_hbm.1, bf16[2,64,1024]{2,1,0:T(8,128)(2,1)} %ck_hbm.1, ...), custom_call_target="tpu_custom_call" | custom-call | tf_op jit(solution)/shard_map/attend/pallas_call | solution.py:295
  75.1 1.0 %put_out.1 = (bf16[2,32,8192]{2,1,0:T(8,128)(2,1)}, bf16[2,4,2048]{2,1,0:T(4,128)(2,1)}, bf16[2,2,2048]{2,1,0:T(2,128)(2,1)}) custom-call(bf16[2,32,8192]{2,1,0:T(8,128)(2,1)S(1)} %get-tuple-element.6.refs_0_, bf16[2,4,2048]{2,1,0:T(4,128)(2,1)S(1)} %get-tuple-element.7.refs_1_, bf16[2,2,2048]{2,1,0:T(2,128)(2,1)S(1)} %get-tuple-element.8.refs_2_), custom_call_target="tpu_custom_call" | custom-call | tf_op jit(solution)/shard_map/put_out/pallas_call | solution.py:319

commit v4 on v3

--- a/solution.py
+++ b/solution.py
@@ -58,8 +58,6 @@
         pltpu.make_async_copy(sv_hbm, s_st.at[:, 1], load_sem.at[3]),
         pltpu.make_async_copy(q_hbm, q_st, load_sem.at[4]),
     ]
-    for copy in loads:
-        copy.start()
 
     partner = (grp, place(x, z, 1 - core))
     above, below = (grp, place(x, z + 1, core)), (grp, place(x, z - 1, core))
@@ -67,6 +65,9 @@
     barrier = pltpu.get_barrier_semaphore()
     for near in (above, below, across, partner):
         pl.semaphore_signal(barrier, inc=1, device_id=near, device_id_type=MESH)
+
+    for copy in loads:
+        copy.start()
 
     def tell(level):
         pl.semaphore_signal(chain.at[0, level], inc=1, device_id=above, device_id_type=MESH)
@@ -142,18 +143,18 @@
         copy.wait()
     pl.semaphore_wait(barrier, 4)
     tell(0)
-    give(2, 4, 1)
+    give(2, 4)
     hear(0)
     tell(1)
-    give(3, 5, 6, 8)
+    give(6, 8, 3, 5)
     hear(1)
     tell(2)
-    give(7, 9, 10, 12)
+    give(10, 12, 7, 9)
     hear(2)
     tell(3)
-    give(11, 13, 14)
+    give(14, 11, 13)
     hear(3)
-    give(15)
+    give(15, 1)
     loads[4].wait()
     for k in reversed(range(1, OWNERS)):
         q_copy(k).start()
@@ -253,10 +254,9 @@
         return carry
 
     lax.fori_loop(0, OWNERS - 1, step, 0)
+    attend(0)
     o_copy(1).start()
-    attend(0)
     mine = pltpu.make_async_copy(o_st.at[0], out_ref.at[x, :, cols(z, WIDTH)], own_sem.at[0])
-    mine.start()
 
     for k in range(1, OWNERS):
         c_copy(k).wait_send()
@@ -265,6 +265,7 @@
     for k in range(OWNERS):
         for copy in forward(k):
             copy.wait_send()
+    mine.start()
     for k in range(1, OWNERS):
         o_copy(k).wait()
     mine.wait()

time: 76.2 us -> 76 us (level)
  no operation moved by 1% of the time
where the time goes in v4:
time: 76 us; the launch traced here: 75.9 us
  Pallas kernels  75.3 us (99%)
    pallas_call x1, Pallas kernels, on_device(): pl.pallas_call(kernel, out_shape=tuple((pltpu.VMEM(shape, jnp.bfloat16) f...  74.3 us

profile of v4, /device:TPU:8, one launch (start us, length us, event | category | flops | bytes accessed | tf_op | source)
XLA Modules:
  0.0 75.9 jit_solution(1648397673707372467)
XLA Ops:
  0.6 74.3 %attend.1 = (bf16[2,32,8192]{2,1,0:T(8,128)(2,1)S(1)}, bf16[2,4,2048]{2,1,0:T(4,128)(2,1)S(1)}, bf16[2,2,2048]{2,1,0:T(2,128)(2,1)S(1)}) custom-call(s32[2]{0:T(128)} %plen_ref.1, bf16[2,32,8192]{2,1,0:T(8,128)(2,1)} %q_hbm.1, bf16[2,32,1024]{2,1,0:T(8,128)(2,1)} %sk_hbm.1, bf16[2,32,1024]{2,1,0:T(8,128)(2,1)} %sv_hbm.1, bf16[2,64,1024]{2,1,0:T(8,128)(2,1)} %ck_hbm.1, ...), custom_call_target="tpu_custom_call" | custom-call | tf_op jit(solution)/shard_map/attend/pallas_call | solution.py:296
  74.9 1.0 %put_out.1 = (bf16[2,32,8192]{2,1,0:T(8,128)(2,1)}, bf16[2,4,2048]{2,1,0:T(4,128)(2,1)}, bf16[2,2,2048]{2,1,0:T(2,128)(2,1)}) custom-call(bf16[2,32,8192]{2,1,0:T(8,128)(2,1)S(1)} %get-tuple-element.6.refs_0_, bf16[2,4,2048]{2,1,0:T(4,128)(2,1)S(1)} %get-tuple-element.7.refs_1_, bf16[2,2,2048]{2,1,0:T(2,128)(2,1)S(1)} %get-tuple-element.8.refs_2_), custom_call_target="tpu_custom_call" | custom-call | tf_op jit(solution)/shard_map/put_out/pallas_call | solution.py:320

commit v5 on v4

--- a/solution.py
+++ b/solution.py
@@ -139,10 +139,10 @@
             c_copy(k).start()
             s_copy(k).start()
 
+    pl.semaphore_wait(barrier, 4)
+    tell(0)
     for copy in loads[:4]:
         copy.wait()
-    pl.semaphore_wait(barrier, 4)
-    tell(0)
     give(2, 4)
     hear(0)
     tell(1)

time: 76 us -> 76 us (level)
  no operation moved by 1% of the time
where the time goes in v5:
time: 76 us; the launch traced here: 75.9 us
  Pallas kernels  75.3 us (99%)
    pallas_call x1, Pallas kernels, on_device(): pl.pallas_call(kernel, out_shape=tuple((pltpu.VMEM(shape, jnp.bfloat16) f...  74.3 us

profile of v5, /device:TPU:8, one launch (start us, length us, event | category | flops | bytes accessed | tf_op | source)
XLA Modules:
  0.0 75.9 jit_solution(8524272406887318084)
XLA Ops:
  0.6 74.3 %attend.1 = (bf16[2,32,8192]{2,1,0:T(8,128)(2,1)S(1)}, bf16[2,4,2048]{2,1,0:T(4,128)(2,1)S(1)}, bf16[2,2,2048]{2,1,0:T(2,128)(2,1)S(1)}) custom-call(s32[2]{0:T(128)} %plen_ref.1, bf16[2,32,8192]{2,1,0:T(8,128)(2,1)} %q_hbm.1, bf16[2,32,1024]{2,1,0:T(8,128)(2,1)} %sk_hbm.1, bf16[2,32,1024]{2,1,0:T(8,128)(2,1)} %sv_hbm.1, bf16[2,64,1024]{2,1,0:T(8,128)(2,1)} %ck_hbm.1, ...), custom_call_target="tpu_custom_call" | custom-call | tf_op jit(solution)/shard_map/attend/pallas_call | solution.py:296
  74.9 1.0 %put_out.1 = (bf16[2,32,8192]{2,1,0:T(8,128)(2,1)}, bf16[2,4,2048]{2,1,0:T(4,128)(2,1)}, bf16[2,2,2048]{2,1,0:T(2,128)(2,1)}) custom-call(bf16[2,32,8192]{2,1,0:T(8,128)(2,1)S(1)} %get-tuple-element.6.refs_0_, bf16[2,4,2048]{2,1,0:T(4,128)(2,1)S(1)} %get-tuple-element.7.refs_1_, bf16[2,2,2048]{2,1,0:T(2,128)(2,1)S(1)} %get-tuple-element.8.refs_2_), custom_call_target="tpu_custom_call" | custom-call | tf_op jit(solution)/shard_map/put_out/pallas_call | solution.py:320
